TPU v7x, 32 devices: a whole 2x2x4 slice. The times are simulated.
32 devices in a mesh: leaf: 2 (over core), row: 4 (over y, x), col: 4 (over z).
Axes of the slice: x: 2, y: 2, z: 4, core: 2. Of those that a mesh axis runs over, the one named last changes fastest.
Arguments:
- rhs_leaf: bfloat16 [2, 8, 64, 2048], P('leaf', None, None, 'col'), may hold values from -6 to 6
- dinv_leaf: bfloat16 [2, 8, 2048, 2048], P('leaf', None, 'row', 'col'), as said below
- panel_leaf: bfloat16 [2, 8, 1024, 2048], P('leaf', None, 'col', 'row'), may hold values from -0.0625 to 0.0625
- counts: int32 [2, 8], P('leaf'), may hold values from 256 to 2048, as said below
- row_index: int32 [2, 8, 1024], P('leaf'), may hold values from 0 to 4095, as said below
- rhs_root: bfloat16 [64, 4096], P(None, 'col'), may hold values from -6 to 6
- dinv_root: bfloat16 [4096, 4096], P(('leaf', 'row')), as said below
Outputs:
- y_leaf: bfloat16 [2, 8, 64, 2048], P('leaf', None, None, 'row')
- y_root: bfloat16 [64, 4096], P(None, ('leaf', 'row'))
Inputs may be any that keep to these rules, and one draw needn't show every extreme that they name: `counts`: each subtree supernode has at least 256 columns; at least one supernode of every draw has all 2048. `row_index`: within one supernode the 1024 entries are distinct and increasing. `dinv_leaf`: each [2048, 2048] block is lower triangular with a nonzero diagonal. `dinv_root`: lower triangular with a nonzero diagonal.
All inputs are finite; a program needn't handle non-finite values.
Results may differ from a plain program's by a relative error of at most 0.0053.
Values may be sent and summed in bfloat16 or wider, within the bound.
No kernel may reach another device: no remote copies, remote signals or barrier semaphores. Data moves between devices by JAX's collectives and lax.ppermute only.
A program may use at most 64 MiB of HBM per device.

v0:
```python
import jax
import jax.numpy as jnp
from jax import lax
from jax.sharding import PartitionSpec as P


def local(rhs_leaf, dinv_leaf, panel_leaf, counts, row_index, rhs_root, dinv_root):
    width_col = rhs_leaf.shape[3]
    width_row = dinv_leaf.shape[2]
    panel_rows = panel_leaf.shape[2]
    columns = rhs_root.shape[0]
    sep_width = rhs_root.shape[1] * lax.axis_size("col")
    limit = counts[0][:, None, None]
    col_slots = lax.axis_index("col") * width_col + lax.iota(jnp.int32, width_col)
    masked = jnp.where(col_slots[None, None, :] < limit, rhs_leaf[0], jnp.zeros((), jnp.bfloat16))
    partial_value = jnp.einsum(
        "kbj,kij->kbi", masked, dinv_leaf[0], preferred_element_type=jnp.float32
    )
    summed = lax.psum(partial_value, "col")
    row_slots = lax.axis_index("row") * width_row + lax.iota(jnp.int32, width_row)
    live_rows = (row_slots[None, None, :] < limit).astype(jnp.float32)
    solved = (summed * live_rows).astype(jnp.bfloat16)
    update = jnp.einsum("kbi,kri->kbr", solved, panel_leaf[0], preferred_element_type=jnp.float32)
    offset = lax.axis_index("col") * panel_rows
    targets = lax.dynamic_slice_in_dim(row_index[0], offset, panel_rows, 1)
    flat_update = jnp.transpose(update, (1, 0, 2)).reshape(columns, -1)
    accum = jnp.zeros((columns, sep_width), jnp.float32).at[:, targets.reshape(-1)].add(flat_update)
    piece = lax.psum_scatter(accum, "col", scatter_dimension=1, tiled=True)
    share = lax.psum(piece, ("leaf", "row"))
    reduced = (rhs_root.astype(jnp.float32) - share).astype(jnp.bfloat16)
    whole_reduced = lax.all_gather(reduced, "col", axis=1, tiled=True)
    y_root = jnp.dot(whole_reduced, dinv_root.T, preferred_element_type=jnp.float32).astype(
        jnp.bfloat16
    )
    return (solved[None], y_root)


def solution(mesh):
    in_specs = (
        P("leaf", None, None, "col"),
        P("leaf", None, "row", "col"),
        P("leaf", None, "col", "row"),
        P("leaf", None),
        P("leaf", None, None),
        P(None, "col"),
        P(("leaf", "row"), None),
    )
    out_specs = (P("leaf", None, None, "row"), P(None, ("leaf", "row")))
    return jax.shard_map(local, mesh=mesh, in_specs=in_specs, out_specs=out_specs, check_vma=False)
```

profile of v0, /device:TPU:0, one launch (start us, length us, event | category | flops | bytes accessed | tf_op | source)
XLA Modules:
  0.0 218.8 jit_solution(5079778243573968000)
XLA Ops:
  7.2 0.0 copy-start
  7.2 0.0 all-reduce.3.cloned.1.call-start
  7.2 0.9 compare_convert_fusion
  8.1 4.7 %fusion = f32[8,64,512]{2,1,0:T(8,128)} fusion(bf16[1,8,512,512]{3,2,1,0:T(8,128)(2,1)} %param.8, bf16[1,8,64,512]{3,2,1,0:T(8,128)(2,1)} %param.7, pred[8,512]{1,0:T(8,128)(4,1)S(1)} %get-tuple-element.3), kind=kOutput, calls=%fused_computation.1 | convolution fusion | flops 268697600 | bytes 5771264 | tf_op jit(solution)/shard_map/kbj,kij->kbi/dot_general | solution.py:16
  12.8 0.0 all-reduce.3.cloned.1.call-update
  12.8 0.0 reduce-scatter.2.cloned.1.call-start
  12.9 0.7 dynamic-slice_bitcast_fusion
  13.6 54.0 %all-reduce.3.cloned.1.call-done = f32[8,64,512]{2,1,0:T(8,128)} async-done(((f32[8,64,512]{2,1,0:T(8,128)}), f32[8,64,512]{2,1,0:T(8,128)}) %all-reduce.3.cloned.1.call-update) | async-done | bytes 1048592 | tf_op jit(solution)/shard_map/psum | solution.py:19
  67.6 0.0 copy-done
  67.6 2.0 fusion.4
  69.6 0.1 copy.13
  69.7 1.3 copy.12
  71.0 0.0 copy-start.2
  71.0 0.0 copy-start.1
  71.0 13.3 %scatter_custom_fusion = f32[64,4096]{0,1:T(8,128)} fusion(s32[2048]{0:T(1024)S(1)} %bitcast.29, f32[2048,64]{1,0:T(8,128)} %copy.12, f32[]{:T(128)} %constant.7.clone.1), kind=kCustom, calls=%fused_computation.7 | custom fusion | flops 131072 | bytes 1049088 | tf_op jit(solution)/shard_map/scatter-add | solution.py:27
  84.3 0.0 reduce-scatter.2.cloned.1.call-update
  84.3 0.0 all-reduce.5.cloned.1.call-start
  84.4 0.0 copy-done.2
  84.4 0.2 copy.10
  84.6 42.8 %reduce-scatter.2.cloned.1.call-done = f32[64,1024]{0,1:T(8,128)} async-done(((f32[64,4096]{0,1:T(8,128)}), f32[64,1024]{0,1:T(8,128)}) %reduce-scatter.2.cloned.1.call-update) | async-done | bytes 262160 | tf_op jit(solution)/shard_map/reduce_scatter | solution.py:28
  127.4 0.0 all-reduce.5.cloned.1.call-update
  127.4 0.0 copy-done.1
  127.4 0.9 fusion.11
  128.4 56.2 %all-reduce.5.cloned.1.call-done = f32[64,1024]{0,1:T(8,128)} async-done(((f32[64,1024]{0,1:T(8,128)}), f32[64,1024]{0,1:T(8,128)}) %all-reduce.5.cloned.1.call-update) | async-done | bytes 262160 | tf_op jit(solution)/shard_map/psum | solution.py:29
  184.5 1.1 subtract_convert_fusion
  185.6 22.4 %all_gather.3 = bf16[64,4096]{0,1:T(8,128)(2,1)S(1)} all-gather(bf16[64,1024]{0,1:T(8,128)(2,1)S(1)} %subtract_convert_fusion), channel_id=1, replica_groups=mesh['leaf'=2,'row'=4,'col'=4] {'col'}, dimensions={1}, use_global_device_ids=true | all-gather | bytes 655360 | tf_op jit(solution)/shard_map/all_gather | solution.py:31
  208.0 4.2 %convolution_convert_fusion = bf16[64,512]{1,0:T(8,128)(2,1)} fusion(bf16[64,4096]{0,1:T(8,128)(2,1)S(1)} %all_gather.3, bf16[512,4096]{1,0:T(8,128)(2,1)} %param.13), kind=kOutput, calls=%fused_computation.6 | convolution fusion | flops 268468224 | bytes 4784128 | tf_op jit(solution)/shard_map/dot_general | solution.py:32
  (3 shorter events, 0.0 us)
Async XLA Ops:
  7.2 60.5 %copy-start = (bf16[1,8,256,512]{3,2,1,0:T(8,128)(2,1)S(1)}, bf16[1,8,256,512]{3,2,1,0:T(8,128)(2,1)}, u32[]{:S(2)}) copy-start(bf16[1,8,256,512]{3,2,1,0:T(8,128)(2,1)} %param.9) | copy-start | bytes 6291460
  7.2 60.4 %all-reduce.3.cloned.1.call-start = ((), (), s32[]{:S(2)}) async-start(), calls=%async_computation.1 | async-start | bytes 2097152 | tf_op jit(solution)/shard_map/psum | solution.py:19
  12.8 114.6 %reduce-scatter.2.cloned.1.call-start = ((), (), s32[]{:S(2)}) async-start(), calls=%async_computation.2 | async-start | bytes 2621440 | tf_op jit(solution)/shard_map/reduce_scatter | solution.py:28
  71.0 13.4 %copy-start.2 = (bf16[64,1024]{1,0:T(8,128)(2,1)S(1)}, bf16[64,1024]{1,0:T(8,128)(2,1)}, u32[]{:S(2)}) copy-start(bf16[64,1024]{1,0:T(8,128)(2,1)} %param.12) | copy-start | bytes 393220
  71.0 56.5 %copy-start.1 = (f32[8,64,512]{2,1,0:T(8,128)S(1)}, f32[8,64,512]{2,1,0:T(8,128)}, u32[]{:S(2)}) copy-start(f32[8,64,512]{2,1,0:T(8,128)} %all-reduce.3.cloned.1.call-done) | copy-start | bytes 3145732
  84.3 100.2 %all-reduce.5.cloned.1.call-start = ((), (), s32[]{:S(2)}) async-start(), calls=%async_computation.3 | async-start | bytes 1048576 | tf_op jit(solution)/shard_map/psum | solution.py:29
Sparse Core Ops, SparseCore 0:
  13.0 54.6 all-reduce.2
  84.5 42.8 reduce-scatter.1
  130.5 53.9 all-reduce.4
where the time goes:
time: 219 us
  waiting for transfers between devices  153 us (70%)
  blocking collectives  22.4 us (10%)
  other arithmetic  16.2 us (7%)
  between operations  13.8 us (6%)
  matrix products  10.9 us (5%)
  local copies, waits for them, and re-layouts  2.27 us (1%)
    psum x1, waiting for transfers between devices, local(): share = lax.psum(piece, ('leaf', 'row'))  56.2 us
    psum x1, waiting for transfers between devices, local(): summed = lax.psum(partial_value, 'col')  54 us
    reduce_scatter x1, waiting for transfers between devices, local(): piece = lax.psum_scatter(accum, 'col', scatter_dimension=1, tiled=True)  42.8 us
    all_gather x1, blocking collectives, local(): whole_reduced = lax.all_gather(reduced, 'col', axis=1, tiled=True)  22.4 us
    scatter-add x1, other arithmetic, local(): jnp.zeros((columns, sep_width), jnp.float32).at[:, targets.reshape(-1)]  13.3 us
    dot_general x1, matrix products, local(): jnp.einsum('kbj,kij->kbi', masked, dinv_leaf[0], preferred_element_type=j...  4.71 us
  transfers between devices with their start and end apart: 3, of which 3 were waited for; matrix products, arithmetic and copies ran while one was open for 1% of the time, Pallas kernels for 0%

commit v1 on v0

--- a/solution.py
+++ b/solution.py
@@ -16,7 +16,7 @@
     partial_value = jnp.einsum(
         "kbj,kij->kbi", masked, dinv_leaf[0], preferred_element_type=jnp.float32
     )
-    summed = lax.psum(partial_value, "col")
+    summed = lax.all_gather(partial_value, axis_name="col").sum(axis=0)
     row_slots = lax.axis_index("row") * width_row + lax.iota(jnp.int32, width_row)
     live_rows = (row_slots[None, None, :] < limit).astype(jnp.float32)
     solved = (summed * live_rows).astype(jnp.bfloat16)

time: 219 us -> 251 us (1.15)
  waiting for transfers between devices: 153 us -> 181 us
  other arithmetic: 16.2 us -> 18.9 us
    all_gather x0 -> x1, waiting for transfers between devices: none -> 82.8 us  [local(): summed = lax.all_gather(partial_value, axis_name='col').sum(axis=0)]
    psum x1 -> x0, waiting for transfers between devices: 54 us -> none  [local(): summed = lax.psum(partial_value, 'col')]
    reduce_sum x0 -> x1, other arithmetic: none -> 2.79 us  [local(): summed = lax.all_gather(partial_value, axis_name='col').sum(axis=0)]
where the time goes in v1:
time: 251 us; the launch traced here: 250 us
  waiting for transfers between devices  181 us (72%)
  blocking collectives  22.4 us (9%)
  other arithmetic  18.9 us (8%)
  between operations  13.8 us (5%)
  matrix products  9.69 us (4%)
  local copies, waits for them, and re-layouts  4.12 us (2%)
    all_gather x1, waiting for transfers between devices, local(): summed = lax.all_gather(partial_value, axis_name='col').sum(axis=0)  82.8 us
    psum x1, waiting for transfers between devices, local(): share = lax.psum(piece, ('leaf', 'row'))  56.2 us
    reduce_scatter x1, waiting for transfers between devices, local(): piece = lax.psum_scatter(accum, 'col', scatter_dimension=1, tiled=True)  42 us
    all_gather x1, blocking collectives, local(): whole_reduced = lax.all_gather(reduced, 'col', axis=1, tiled=True)  22.4 us
    scatter-add x1, other arithmetic, local(): jnp.zeros((columns, sep_width), jnp.float32).at[:, targets.reshape(-1)]  13.2 us
  transfers between devices with their start and end apart: 3, of which 3 were waited for; matrix products, arithmetic and copies ran while one was open for 1% of the time, Pallas kernels for 0%

profile of v1, /device:TPU:0, one launch (start us, length us, event | category | flops | bytes accessed | tf_op | source)
XLA Modules:
  0.0 250.1 jit_solution(16833162208570134938)
XLA Ops:
  7.2 0.0 copy-start
  7.2 0.0 all-gather.3.cloned.1.call-start
  7.2 0.9 compare_convert_fusion
  8.1 4.7 %fusion = f32[8,64,512]{2,1,0:T(8,128)} fusion(bf16[1,8,512,512]{3,2,1,0:T(8,128)(2,1)} %param.8, bf16[1,8,64,512]{3,2,1,0:T(8,128)(2,1)} %param.7, pred[8,512]{1,0:T(8,128)(4,1)S(1)} %get-tuple-element.3), kind=kOutput, calls=%fused_computation.1 | convolution fusion | flops 268697600 | bytes 5771264 | tf_op jit(solution)/shard_map/kbj,kij->kbi/dot_general | solution.py:16
  12.8 0.0 all-gather.3.cloned.1.call-update
  12.8 0.0 reduce-scatter.2.cloned.1.call-start
  12.9 0.7 dynamic-slice_bitcast_fusion
  13.6 82.8 %all-gather.3.cloned.1.call-done = f32[32,64,512]{2,1,0:T(8,128)} async-done(((f32[8,64,512]{2,1,0:T(8,128)}), f32[32,64,512]{2,1,0:T(8,128)}) %all-gather.3.cloned.1.call-update) | async-done | bytes 4194320 | tf_op jit(solution)/shard_map/all_gather | solution.py:19
  96.5 2.8 %reduce_sum.11 = f32[8,64,512]{2,1,0:T(8,128)S(1)} reduce(f32[4,8,64,512]{3,2,1,0:T(8,128)} %bitcast.30, f32[]{:T(128)} %constant.5.clone.1), dimensions={0}, to_apply=%region_0.1 | reduce | flops 786432 | bytes 5242884 | tf_op jit(solution)/shard_map/reduce_sum | solution.py:19
  99.2 0.0 copy-done
  99.3 0.7 fusion.4
  100.0 0.9 copy.16
  100.9 2.4 copy.15
  103.2 0.0 copy-start.1
  103.2 13.2 %scatter_custom_fusion = f32[64,4096]{0,1:T(8,128)} fusion(s32[2048]{0:T(1024)S(1)} %bitcast.33, f32[2048,64]{1,0:T(8,128)} %copy.15, f32[]{:T(128)} %constant.5.clone.1), kind=kCustom, calls=%fused_computation.10 | custom fusion | flops 131072 | bytes 1049088 | tf_op jit(solution)/shard_map/scatter-add | solution.py:27
  116.5 0.0 reduce-scatter.2.cloned.1.call-update
  116.5 0.0 all-reduce.2.cloned.1.call-start
  116.6 0.0 copy-done.1
  116.6 0.2 copy.13
  116.7 42.0 %reduce-scatter.2.cloned.1.call-done = f32[64,1024]{0,1:T(8,128)} async-done(((f32[64,4096]{0,1:T(8,128)}), f32[64,1024]{0,1:T(8,128)}) %reduce-scatter.2.cloned.1.call-update) | async-done | bytes 262160 | tf_op jit(solution)/shard_map/reduce_scatter | solution.py:28
  158.8 0.0 all-reduce.2.cloned.1.call-update
  158.8 0.9 fusion.7
  159.7 56.2 %all-reduce.2.cloned.1.call-done = f32[64,1024]{0,1:T(8,128)} async-done(((f32[64,1024]{0,1:T(8,128)}), f32[64,1024]{0,1:T(8,128)}) %all-reduce.2.cloned.1.call-update) | async-done | bytes 262160 | tf_op jit(solution)/shard_map/psum | solution.py:29
  215.9 1.1 subtract_convert_fusion
  217.0 22.4 %all_gather.11 = bf16[64,4096]{0,1:T(8,128)(2,1)S(1)} all-gather(bf16[64,1024]{0,1:T(8,128)(2,1)S(1)} %subtract_convert_fusion), channel_id=1, replica_groups=mesh['leaf'=2,'row'=4,'col'=4] {'col'}, dimensions={1}, use_global_device_ids=true | all-gather | bytes 655360 | tf_op jit(solution)/shard_map/all_gather | solution.py:31
  239.4 4.2 %convolution_convert_fusion = bf16[64,512]{1,0:T(8,128)(2,1)} fusion(bf16[64,4096]{0,1:T(8,128)(2,1)S(1)} %all_gather.11, bf16[512,4096]{1,0:T(8,128)(2,1)} %param.13), kind=kOutput, calls=%fused_computation.6 | convolution fusion | flops 268468224 | bytes 4784128 | tf_op jit(solution)/shard_map/dot_general | solution.py:32
  (3 shorter events, 0.0 us)
Async XLA Ops:
  7.2 92.1 %copy-start = (bf16[1,8,256,512]{3,2,1,0:T(8,128)(2,1)S(1)}, bf16[1,8,256,512]{3,2,1,0:T(8,128)(2,1)}, u32[]{:S(2)}) copy-start(bf16[1,8,256,512]{3,2,1,0:T(8,128)(2,1)} %param.9) | copy-start | bytes 6291460
  7.2 89.3 %all-gather.3.cloned.1.call-start = ((), (), s32[]{:S(2)}) async-start(), calls=%async_computation.3 | async-start | bytes 5242880 | tf_op jit(solution)/shard_map/all_gather | solution.py:19
  12.8 145.9 %reduce-scatter.2.cloned.1.call-start = ((), (), s32[]{:S(2)}) async-start(), calls=%async_computation.1 | async-start | bytes 2621440 | tf_op jit(solution)/shard_map/reduce_scatter | solution.py:28
  103.2 13.3 %copy-start.1 = (bf16[64,1024]{1,0:T(8,128)(2,1)S(1)}, bf16[64,1024]{1,0:T(8,128)(2,1)}, u32[]{:S(2)}) copy-start(bf16[64,1024]{1,0:T(8,128)(2,1)} %param.12) | copy-start | bytes 393220
  116.5 99.4 %all-reduce.2.cloned.1.call-start = ((), (), s32[]{:S(2)}) async-start(), calls=%async_computation.2 | async-start | bytes 1048576 | tf_op jit(solution)/shard_map/psum | solution.py:29
Sparse Core Ops, SparseCore 0:
  13.0 83.4 all-gather.2
  116.6 42.1 reduce-scatter.1
  161.9 53.9 all-reduce.1
